TPU v7x, 32 devices: a whole 2x2x4 slice. The times are simulated.
32 devices in a mesh: clip: 4 (over y, x), head: 8 (over z, core).
Axes of the slice: x: 2, y: 2, z: 4, core: 2. Of those that a mesh axis runs over, the one named last changes fastest.
Arguments:
- queries: bfloat16 [8192, 4096], P(('clip', 'head')), may hold values from -6 to 6
- key_rows: bfloat16 [8192, 4096], P(('clip', 'head')), may hold values from -6 to 6
- value_rows: bfloat16 [8192, 4096], P(('clip', 'head')), may hold values from -6 to 6
- query_tangent: bfloat16 [8192, 4096], P(('clip', 'head')), may hold values from -6 to 6
- key_tangent: bfloat16 [8192, 4096], P(('clip', 'head')), may hold values from -6 to 6
- value_tangent: bfloat16 [8192, 4096], P(('clip', 'head')), may hold values from -6 to 6
- partners: int32 [8, 2], replicated, may hold values from 0 to 7, as said below
- cotangent: bfloat16 [8192, 3072], P('clip'), may hold values from -6 to 6
Outputs:
- attended: bfloat16 [8192, 4096], P(('clip', 'head'))
- attended_tangent: bfloat16 [8192, 4096], P(('clip', 'head'))
- weight_grad: float32 [3072, 4096], P('clip', 'head')
Inputs may be any that keep to these rules, and one draw needn't show every extreme that they name: `partners`: for clip c the two entries are distinct clips (c - d) mod 8 with 1 <= d <= 2 + c % 2.
All inputs are finite; a program needn't handle non-finite values.
Results may differ from a plain program's by a relative error of at most 0.0051.
Values may be sent and summed in bfloat16 or wider, within the bound.
A program may use at most 192 MiB of HBM per device.

v0:
```python
import jax
import jax.numpy as jnp
from jax import lax
from jax.sharding import PartitionSpec as P

HDIM = 128
CLIP = 1024


def shifted(shard, axis, by):
    length = lax.axis_size(axis)
    return lax.ppermute(shard, axis, [(i, (i + by) % length) for i in range(length)])


def as_sent(shard):
    return jax.tree.map(lambda a: a.astype(jnp.bfloat16) if a.dtype == jnp.float32 else a, shard)


def attend_block(query_block, qtan_block, key_win, value_win, ktan_win, vtan_win):
    score_scale = query_block.shape[-1] ** (-0.5)
    scores = (
        jnp.einsum("qhd,khd->hqk", query_block, key_win, preferred_element_type=jnp.float32)
        * score_scale
    )
    score_tan = (
        jnp.einsum("qhd,khd->hqk", qtan_block, key_win, preferred_element_type=jnp.float32)
        + jnp.einsum("qhd,khd->hqk", query_block, ktan_win, preferred_element_type=jnp.float32)
    ) * score_scale
    row_max = jnp.max(scores, axis=-1, keepdims=True)
    raw_weights = jnp.exp(scores - row_max)
    row_total = jnp.sum(raw_weights, axis=-1, keepdims=True)
    probability = raw_weights / row_total
    tangent_mean = jnp.sum(probability * score_tan, axis=-1, keepdims=True)
    prob_tangent = probability * (score_tan - tangent_mean)
    prob_low = probability.astype(jnp.bfloat16)
    tangent_low = prob_tangent.astype(jnp.bfloat16)
    result_out = jnp.einsum("hqk,khd->qhd", prob_low, value_win, preferred_element_type=jnp.float32)
    tangent_out = jnp.einsum(
        "hqk,khd->qhd", tangent_low, value_win, preferred_element_type=jnp.float32
    ) + jnp.einsum("hqk,khd->qhd", prob_low, vtan_win, preferred_element_type=jnp.float32)
    return (result_out.astype(jnp.bfloat16), tangent_out.astype(jnp.bfloat16))


def on_device(
    queries, key_rows, value_rows, query_tangent, key_tangent, value_tangent, partners, cotangent
):
    clip_count = lax.axis_size("clip")
    regrouped = (
        lax.all_to_all(queries, "head", split_axis=1, concat_axis=0, tiled=True),
        lax.all_to_all(key_rows, "head", split_axis=1, concat_axis=0, tiled=True),
        lax.all_to_all(value_rows, "head", split_axis=1, concat_axis=0, tiled=True),
        lax.all_to_all(query_tangent, "head", split_axis=1, concat_axis=0, tiled=True),
        lax.all_to_all(key_tangent, "head", split_axis=1, concat_axis=0, tiled=True),
        lax.all_to_all(value_tangent, "head", split_axis=1, concat_axis=0, tiled=True),
    )
    query_h, key_h, value_h, qtan_h, ktan_h, vtan_h = regrouped
    prev_key, prev_value, prev_ktan, prev_vtan = shifted(
        (key_h, value_h, ktan_h, vtan_h), "clip", 1
    )
    window_key = jnp.concatenate([prev_key, key_h], axis=0)
    window_value = jnp.concatenate([prev_value, value_h], axis=0)
    window_ktan = jnp.concatenate([prev_ktan, ktan_h], axis=0)
    window_vtan = jnp.concatenate([prev_vtan, vtan_h], axis=0)
    group_rows = query_h.shape[0]
    cols_here = query_h.shape[1]
    heads_here = cols_here // HDIM
    clips_here = group_rows // CLIP
    total_clips = clips_here * clip_count
    first_clip = lax.axis_index("clip") * clips_here
    block_rows = min(512, CLIP)

    def one_clip(within):
        partner_row = lax.dynamic_slice_in_dim(partners, first_clip + within, 1, 0)[0]
        slots_here = (partner_row - first_clip + clips_here) % total_clips
        slot_list = [clips_here + within, slots_here[0], slots_here[1]]

        def window(array):
            parts = [lax.dynamic_slice_in_dim(array, slot * CLIP, CLIP, 0) for slot in slot_list]
            return jnp.concatenate(parts, axis=0).reshape(3 * CLIP, heads_here, HDIM)

        key_win = window(window_key)
        value_win = window(window_value)
        ktan_win = window(window_ktan)
        vtan_win = window(window_vtan)
        clip_start = within * CLIP
        query_clip = lax.dynamic_slice_in_dim(query_h, clip_start, CLIP, 0).reshape(
            CLIP, heads_here, HDIM
        )
        qtan_clip = lax.dynamic_slice_in_dim(qtan_h, clip_start, CLIP, 0).reshape(
            CLIP, heads_here, HDIM
        )
        outputs = []
        tangents = []
        for block in range(CLIP // block_rows):
            lower = block * block_rows
            result_out, tangent_out = attend_block(
                query_clip[lower : lower + block_rows],
                qtan_clip[lower : lower + block_rows],
                key_win,
                value_win,
                ktan_win,
                vtan_win,
            )
            outputs.append(result_out.reshape(block_rows, cols_here))
            tangents.append(tangent_out.reshape(block_rows, cols_here))
        return (jnp.concatenate(outputs, axis=0), jnp.concatenate(tangents, axis=0))

    results = lax.map(one_clip, jnp.arange(clips_here, dtype=jnp.int32))
    output_h = results[0].reshape(group_rows, cols_here)
    tangent_h = results[1].reshape(group_rows, cols_here)
    attended, attended_tangent = (
        lax.all_to_all(as_sent(output_h), "head", split_axis=0, concat_axis=1, tiled=True).astype(
            output_h.dtype
        ),
        lax.all_to_all(as_sent(tangent_h), "head", split_axis=0, concat_axis=1, tiled=True).astype(
            tangent_h.dtype
        ),
    )
    partial_term = lax.dot_general(
        cotangent, output_h, (((0,), (0,)), ((), ())), preferred_element_type=jnp.float32
    )
    weight_grad = lax.psum_scatter(partial_term, "clip", scatter_dimension=0, tiled=True)
    return (attended, attended_tangent, weight_grad)


def solution(mesh):
    return jax.shard_map(
        on_device,
        mesh=mesh,
        in_specs=(
            P(("clip", "head"), None),
            P(("clip", "head"), None),
            P(("clip", "head"), None),
            P(("clip", "head"), None),
            P(("clip", "head"), None),
            P(("clip", "head"), None),
            P(),
            P("clip", None),
        ),
        out_specs=(P(("clip", "head"), None), P(("clip", "head"), None), P("clip", "head")),
        check_vma=False,
    )
```

profile of v0, /device:TPU:0, one launch (start us, length us, event | category | flops | bytes accessed | tf_op | source)
XLA Modules:
  0.0 1080.0 jit_solution(4664718953220969203)
XLA Ops:
  11.2 6.4 all-to-all-start.2
  21.7 45.0 %all-to-all-done.2 = bf16[256,8,512]{0,2,1:T(8,128)(2,1)S(1)} async-done(((bf16[256,8,512]{0,2,1:T(8,128)(2,1)}), bf16[256,8,512]{0,2,1:T(8,128)(2,1)S(1)}, u32[]{:S(2)}, u32[]{:S(2)}) %all-to-all-start.2) | async-done | bytes 2097184 | tf_op jit(solution)/shard_map/all_to_all | solution.py:50
  75.1 44.9 %all-to-all-done.4 = bf16[256,8,512]{0,2,1:T(8,128)(2,1)} async-done(((bf16[256,8,512]{0,2,1:T(8,128)(2,1)}), bf16[256,8,512]{0,2,1:T(8,128)(2,1)}, u32[]{:S(2)}, u32[]{:S(2)}) %all-to-all-start.4) | async-done | bytes 2097184 | tf_op jit(solution)/shard_map/all_to_all | solution.py:53
  128.5 45.0 %all-to-all-done.5 = bf16[256,8,512]{0,2,1:T(8,128)(2,1)} async-done(((bf16[256,8,512]{0,2,1:T(8,128)(2,1)}), bf16[256,8,512]{0,2,1:T(8,128)(2,1)}, u32[]{:S(2)}, u32[]{:S(2)}) %all-to-all-start.5) | async-done | bytes 2097184 | tf_op jit(solution)/shard_map/all_to_all | solution.py:54
  181.9 45.0 %all-to-all-done = bf16[256,8,512]{0,2,1:T(8,128)(2,1)} async-done(((bf16[256,8,512]{0,2,1:T(8,128)(2,1)}), bf16[256,8,512]{0,2,1:T(8,128)(2,1)}, u32[]{:S(2)}, u32[]{:S(2)}) %all-to-all-start) | async-done | bytes 2097184 | tf_op jit(solution)/shard_map/all_to_all | solution.py:51
  226.8 4.4 all-to-all-start.1
  235.3 44.9 %all-to-all-done.1 = bf16[256,8,512]{0,2,1:T(8,128)(2,1)} async-done(((bf16[256,8,512]{0,2,1:T(8,128)(2,1)}), bf16[256,8,512]{0,2,1:T(8,128)(2,1)}, u32[]{:S(2)}, u32[]{:S(2)}) %all-to-all-start.1) | async-done | bytes 2097184 | tf_op jit(solution)/shard_map/all_to_all | solution.py:49
  306.8 26.8 %all-to-all-done.3 = bf16[256,8,512]{0,2,1:T(8,128)(2,1)} async-done(((bf16[256,8,512]{0,2,1:T(8,128)(2,1)}), bf16[256,8,512]{0,2,1:T(8,128)(2,1)}, u32[]{:S(2)}, u32[]{:S(2)}) %all-to-all-start.3) | async-done | bytes 2097184 | tf_op jit(solution)/shard_map/all_to_all | solution.py:52
  337.5 4.4 pad_maximum_fusion.5
  342.0 6.5 copy.123
  348.4 33.3 %collective-permute-done.2 = bf16[2048,512]{1,0:T(8,128)(2,1)} collective-permute-done((bf16[2048,512]{1,0:T(8,128)(2,1)}, bf16[2048,512]{1,0:T(8,128)(2,1)}, u32[]{:S(2)}, u32[]{:S(2)}) %collective-permute-start.2) | collective-permute-done | bytes 2097184 | tf_op jit(solution)/shard_map/ppermute | solution.py:12
  381.7 4.4 pad_maximum_fusion.6
  386.2 6.4 copy.125
  392.6 34.1 %collective-permute-done.3 = bf16[2048,512]{1,0:T(8,128)(2,1)} collective-permute-done((bf16[2048,512]{1,0:T(8,128)(2,1)}, bf16[2048,512]{1,0:T(8,128)(2,1)}, u32[]{:S(2)}, u32[]{:S(2)}) %collective-permute-start.3) | collective-permute-done | bytes 2097184 | tf_op jit(solution)/shard_map/ppermute | solution.py:12
  426.7 4.4 pad_maximum_fusion.7
  431.1 6.4 copy.126
  437.5 33.5 %collective-permute-done = bf16[2048,512]{1,0:T(8,128)(2,1)} collective-permute-done((bf16[2048,512]{1,0:T(8,128)(2,1)S(1)}, bf16[2048,512]{1,0:T(8,128)(2,1)}, u32[]{:S(2)}, u32[]{:S(2)}) %collective-permute-start) | collective-permute-done | bytes 2097184 | tf_op jit(solution)/shard_map/ppermute | solution.py:12
  474.8 6.5 copy.120
  481.8 461.5 %while.14 = (s32[]{:T(128)}, bf16[2,1024,512]{2,1,0:T(8,128)(2,1)}, bf16[2,1024,512]{2,1,0:T(8,128)(2,1)}, s32[2]{0:T(128)}, bf16[4096,512]{0,1:T(8,128)(2,1)}, ...) while((s32[]{:T(128)}, bf16[2,1024,512]{2,1,0:T(8,128)(2,1)}, ...), condition=%wide.region_7.8_spmd, body=%wide.region_0.7_spmd.sunk | while | flops 19572197376 | bytes 686934336 | solution.py:108
  506.3 5.0 constant_dynamic-slice_fusion.20
  517.1 13.8 %fusion.128 = (f32[4,512]{1,0:T(4,128)S(1)}, f32[4,512,3072]{2,1,0:T(8,128)}) fusion(bf16[512,4,128]{0,2,1:T(8,128)(2,1)} %bitcast.174, bf16[3072,4,128]{0,2,1:T(8,128)(2,1)S(1)} %bitcast.158), kind=kOutput, calls=%fused_computation.78.clone.1 | convolution fusion | flops 1629490176 | bytes 28844032 | tf_op jit(solution)/shard_map/while/body/eval_jaxpr/sub | solution.py:30
  533.0 11.3 %fusion.134 = f32[4,512,3072]{2,1,0:T(8,128)} fusion(bf16[512,4,128]{0,2,1:T(8,128)(2,1)} %bitcast.170, bf16[3072,4,128]{0,2,1:T(8,128)(2,1)S(1)} %bitcast.159), kind=kOutput, calls=%fused_computation.79.clone.1 | convolution fusion | flops 1610612736 | bytes 28835840 | tf_op jit(solution)/shard_map/while/body/eval_jaxpr/qhd,khd->hqk/dot_general | solution.py:26
  548.2 28.1 %multiply_reduce_fusion.7 = (f32[4,512]{1,0:T(4,128)S(1)}, f32[4,512,3072]{2,1,0:T(8,128)}) fusion(f32[4,512,3072]{2,1,0:T(8,128)} %get-tuple-element.400, f32[4,512]{1,0:T(4,128)S(1)} %get-tuple-element.401, f32[4,512,3072]{2,1,0:T(8,128)} %fusion.134, bf16[512,4,128]{0,2,1:T(8,128)(2,1)} %bitcast.175, bf16[3072,4,128]{0,2,1:T(8,128)(2,1)} %bitcast.166), kind=kOutput, calls=%fused_computation.6.clone.1 | convolution fusion | flops 1642067968 | bytes 79183872 | tf_op jit(solution)/shard_map/while/body/eval_jaxpr/qhd,khd->hqk/dot_general | solution.py:27
  578.3 12.7 %fusion.133 = f32[4,128,512]{2,1,0:T(8,128)} fusion(bf16[3072,4,128]{0,2,1:T(8,128)(2,1)S(1)} %bitcast.168, f32[4,512,3072]{2,1,0:T(8,128)} %get-tuple-element.400, f32[4,512]{1,0:T(4,128)S(1)} %get-tuple-element.401), kind=kOutput, calls=%fused_computation.26.clone.1 | convolution fusion | flops 1623195648 | bytes 29368320 | tf_op jit(solution)/shard_map/while/body/eval_jaxpr/hqk,khd->qhd/dot_general | solution.py:40
  592.3 18.7 %fusion.135 = bf16[4,128,512]{2,1,0:T(8,128)(2,1)} fusion(f32[4,128,512]{2,1,0:T(8,128)S(1)} %copy-done.15, bf16[3072,4,128]{0,2,1:T(8,128)(2,1)S(1)} %bitcast.162, f32[4,512,3072]{2,1,0:T(8,128)} %get-tuple-element.412, f32[4,512]{1,0:T(4,128)S(1)} %get-tuple-element.413, f32[4,512,3072]{2,1,0:T(8,128)} %get-tuple-element.400, ...), kind=kOutput, calls=%fused_computation.40.clone.1 | convolution fusion | flops 1636302848 | bytes 55066624 | tf_op jit(solution)/shard_map/while/body/eval_jaxpr/hqk,khd->qhd/dot_general | solution.py:38
  613.0 11.3 %fusion.131 = f32[4,512,3072]{2,1,0:T(8,128)} fusion(bf16[512,4,128]{0,2,1:T(8,128)(2,1)} %bitcast.171, bf16[3072,4,128]{0,2,1:T(8,128)(2,1)S(1)} %bitcast.160), kind=kOutput, calls=%fused_computation.80.clone.1 | convolution fusion | flops 1610612736 | bytes 28835840 | tf_op jit(solution)/shard_map/while/body/eval_jaxpr/qhd,khd->hqk/dot_general | solution.py:26
  626.4 13.7 %fusion.126 = (f32[4,512]{1,0:T(4,128)S(1)}, f32[4,512,3072]{2,1,0:T(8,128)}) fusion(bf16[512,4,128]{0,2,1:T(8,128)(2,1)} %bitcast.176, bf16[3072,4,128]{0,2,1:T(8,128)(2,1)S(1)} %bitcast.161), kind=kOutput, calls=%fused_computation.77.clone.1 | convolution fusion | flops 1629490176 | bytes 28844032 | tf_op jit(solution)/shard_map/while/body/eval_jaxpr/sub | solution.py:30
  640.1 28.2 %multiply_reduce_fusion.6 = (f32[4,512]{1,0:T(4,128)S(1)}, f32[4,512,3072]{2,1,0:T(8,128)}) fusion(f32[4,512,3072]{2,1,0:T(8,128)} %get-tuple-element.397, f32[4,512]{1,0:T(4,128)S(1)} %get-tuple-element.398, f32[4,512,3072]{2,1,0:T(8,128)} %fusion.131, bf16[512,4,128]{0,2,1:T(8,128)(2,1)} %bitcast.177, bf16[3072,4,128]{0,2,1:T(8,128)(2,1)} %bitcast.167), kind=kOutput, calls=%fused_computation.3.clone.1 | convolution fusion | flops 1642067968 | bytes 79183872 | tf_op jit(solution)/shard_map/while/body/eval_jaxpr/qhd,khd->hqk/dot_general | solution.py:27
  668.3 10.6 fusion.130
  678.9 17.9 %fusion.132 = bf16[4,128,512]{2,1,0:T(8,128)(2,1)S(1)} fusion(f32[4,128,512]{2,1,0:T(8,128)S(1)} %fusion.130, bf16[3072,4,128]{0,2,1:T(8,128)(2,1)S(1)} %bitcast.164, f32[4,512,3072]{2,1,0:T(8,128)} %get-tuple-element.409, f32[4,512]{1,0:T(4,128)S(1)} %get-tuple-element.410, f32[4,512,3072]{2,1,0:T(8,128)} %get-tuple-element.397, ...), kind=kOutput, calls=%fused_computation.41.clone.1 | convolution fusion | flops 1636302848 | bytes 55066624 | tf_op jit(solution)/shard_map/while/body/eval_jaxpr/hqk,khd->qhd/dot_general | solution.py:38
  698.6 11.6 %fusion.129 = bf16[4,128,512]{2,1,0:T(8,128)(2,1)S(1)} fusion(bf16[3072,4,128]{0,2,1:T(8,128)(2,1)} %bitcast.163, f32[4,512,3072]{2,1,0:T(8,128)} %get-tuple-element.400, f32[4,512]{1,0:T(4,128)S(1)} %get-tuple-element.401), kind=kOutput, calls=%fused_computation.38.clone.1 | convolution fusion | flops 1623457792 | bytes 28844032 | tf_op jit(solution)/shard_map/while/body/eval_jaxpr/hqk,khd->qhd/dot_general | solution.py:37
  710.2 10.6 fusion.127
  727.0 5.0 constant_dynamic-slice_fusion.20
  737.8 13.8 %fusion.128 = (f32[4,512]{1,0:T(4,128)S(1)}, f32[4,512,3072]{2,1,0:T(8,128)}) fusion(bf16[512,4,128]{0,2,1:T(8,128)(2,1)} %bitcast.174, bf16[3072,4,128]{0,2,1:T(8,128)(2,1)S(1)} %bitcast.158), kind=kOutput, calls=%fused_computation.78.clone.1 | convolution fusion | flops 1629490176 | bytes 28844032 | tf_op jit(solution)/shard_map/while/body/eval_jaxpr/sub | solution.py:30
  753.7 11.3 %fusion.134 = f32[4,512,3072]{2,1,0:T(8,128)} fusion(bf16[512,4,128]{0,2,1:T(8,128)(2,1)} %bitcast.170, bf16[3072,4,128]{0,2,1:T(8,128)(2,1)S(1)} %bitcast.159), kind=kOutput, calls=%fused_computation.79.clone.1 | convolution fusion | flops 1610612736 | bytes 28835840 | tf_op jit(solution)/shard_map/while/body/eval_jaxpr/qhd,khd->hqk/dot_general | solution.py:26
  768.9 28.1 %multiply_reduce_fusion.7 = (f32[4,512]{1,0:T(4,128)S(1)}, f32[4,512,3072]{2,1,0:T(8,128)}) fusion(f32[4,512,3072]{2,1,0:T(8,128)} %get-tuple-element.400, f32[4,512]{1,0:T(4,128)S(1)} %get-tuple-element.401, f32[4,512,3072]{2,1,0:T(8,128)} %fusion.134, bf16[512,4,128]{0,2,1:T(8,128)(2,1)} %bitcast.175, bf16[3072,4,128]{0,2,1:T(8,128)(2,1)} %bitcast.166), kind=kOutput, calls=%fused_computation.6.clone.1 | convolution fusion | flops 1642067968 | bytes 79183872 | tf_op jit(solution)/shard_map/while/body/eval_jaxpr/qhd,khd->hqk/dot_general | solution.py:27
  799.0 12.7 %fusion.133 = f32[4,128,512]{2,1,0:T(8,128)} fusion(bf16[3072,4,128]{0,2,1:T(8,128)(2,1)S(1)} %bitcast.168, f32[4,512,3072]{2,1,0:T(8,128)} %get-tuple-element.400, f32[4,512]{1,0:T(4,128)S(1)} %get-tuple-element.401), kind=kOutput, calls=%fused_computation.26.clone.1 | convolution fusion | flops 1623195648 | bytes 29368320 | tf_op jit(solution)/shard_map/while/body/eval_jaxpr/hqk,khd->qhd/dot_general | solution.py:40
  812.9 18.7 %fusion.135 = bf16[4,128,512]{2,1,0:T(8,128)(2,1)} fusion(f32[4,128,512]{2,1,0:T(8,128)S(1)} %copy-done.15, bf16[3072,4,128]{0,2,1:T(8,128)(2,1)S(1)} %bitcast.162, f32[4,512,3072]{2,1,0:T(8,128)} %get-tuple-element.412, f32[4,512]{1,0:T(4,128)S(1)} %get-tuple-element.413, f32[4,512,3072]{2,1,0:T(8,128)} %get-tuple-element.400, ...), kind=kOutput, calls=%fused_computation.40.clone.1 | convolution fusion | flops 1636302848 | bytes 55066624 | tf_op jit(solution)/shard_map/while/body/eval_jaxpr/hqk,khd->qhd/dot_general | solution.py:38
  833.7 11.3 %fusion.131 = f32[4,512,3072]{2,1,0:T(8,128)} fusion(bf16[512,4,128]{0,2,1:T(8,128)(2,1)} %bitcast.171, bf16[3072,4,128]{0,2,1:T(8,128)(2,1)S(1)} %bitcast.160), kind=kOutput, calls=%fused_computation.80.clone.1 | convolution fusion | flops 1610612736 | bytes 28835840 | tf_op jit(solution)/shard_map/while/body/eval_jaxpr/qhd,khd->hqk/dot_general | solution.py:26
  847.0 13.7 %fusion.126 = (f32[4,512]{1,0:T(4,128)S(1)}, f32[4,512,3072]{2,1,0:T(8,128)}) fusion(bf16[512,4,128]{0,2,1:T(8,128)(2,1)} %bitcast.176, bf16[3072,4,128]{0,2,1:T(8,128)(2,1)S(1)} %bitcast.161), kind=kOutput, calls=%fused_computation.77.clone.1 | convolution fusion | flops 1629490176 | bytes 28844032 | tf_op jit(solution)/shard_map/while/body/eval_jaxpr/sub | solution.py:30
  860.8 28.2 %multiply_reduce_fusion.6 = (f32[4,512]{1,0:T(4,128)S(1)}, f32[4,512,3072]{2,1,0:T(8,128)}) fusion(f32[4,512,3072]{2,1,0:T(8,128)} %get-tuple-element.397, f32[4,512]{1,0:T(4,128)S(1)} %get-tuple-element.398, f32[4,512,3072]{2,1,0:T(8,128)} %fusion.131, bf16[512,4,128]{0,2,1:T(8,128)(2,1)} %bitcast.177, bf16[3072,4,128]{0,2,1:T(8,128)(2,1)} %bitcast.167), kind=kOutput, calls=%fused_computation.3.clone.1 | convolution fusion | flops 1642067968 | bytes 79183872 | tf_op jit(solution)/shard_map/while/body/eval_jaxpr/qhd,khd->hqk/dot_general | solution.py:27
  889.0 10.6 fusion.130
  899.6 17.9 %fusion.132 = bf16[4,128,512]{2,1,0:T(8,128)(2,1)S(1)} fusion(f32[4,128,512]{2,1,0:T(8,128)S(1)} %fusion.130, bf16[3072,4,128]{0,2,1:T(8,128)(2,1)S(1)} %bitcast.164, f32[4,512,3072]{2,1,0:T(8,128)} %get-tuple-element.409, f32[4,512]{1,0:T(4,128)S(1)} %get-tuple-element.410, f32[4,512,3072]{2,1,0:T(8,128)} %get-tuple-element.397, ...), kind=kOutput, calls=%fused_computation.41.clone.1 | convolution fusion | flops 1636302848 | bytes 55066624 | tf_op jit(solution)/shard_map/while/body/eval_jaxpr/hqk,khd->qhd/dot_general | solution.py:38
  919.3 11.6 %fusion.129 = bf16[4,128,512]{2,1,0:T(8,128)(2,1)S(1)} fusion(bf16[3072,4,128]{0,2,1:T(8,128)(2,1)} %bitcast.163, f32[4,512,3072]{2,1,0:T(8,128)} %get-tuple-element.400, f32[4,512]{1,0:T(4,128)S(1)} %get-tuple-element.401), kind=kOutput, calls=%fused_computation.38.clone.1 | convolution fusion | flops 1623457792 | bytes 28844032 | tf_op jit(solution)/shard_map/while/body/eval_jaxpr/hqk,khd->qhd/dot_general | solution.py:37
  930.8 10.6 fusion.127
  943.3 12.1 %convolution_bitcast_fusion = f32[3072,512]{0,1:T(8,128)} fusion(bf16[2048,512]{1,0:T(8,128)(2,1)} %bitcast.196, bf16[2048,3072]{1,0:T(8,128)(2,1)} %param.17), kind=kOutput, calls=%fused_computation.71 | convolution fusion | flops 6442450944 | bytes 20971520 | tf_op jit(solution)/shard_map/dot_general | solution.py:119
  957.0 53.7 %all_to_all.152 = bf16[8,256,512]{2,1,0:T(8,128)(2,1)} all-to-all(bf16[8,256,512]{2,1,0:T(8,128)(2,1)S(1)} %bitcast.197), channel_id=1, replica_groups=mesh['clip'=4,'head'=8] {'head'}, dimensions={0} | all-to-all | bytes 4194304 | tf_op jit(solution)/shard_map/all_to_all | solution.py:112
  1022.3 41.0 %all-to-all-done.7 = bf16[8,256,512]{2,1,0:T(8,128)(2,1)S(1)} async-done(((bf16[8,256,512]{2,1,0:T(8,128)(2,1)}), bf16[8,256,512]{2,1,0:T(8,128)(2,1)S(1)}, u32[]{:S(2)}, u32[]{:S(2)}) %all-to-all-start.7) | async-done | bytes 2097184 | tf_op jit(solution)/shard_map/all_to_all | solution.py:115
  (133 shorter events, 142.9 us)
Async XLA Ops:
  11.2 55.4 %all-to-all-start.2 = ((bf16[256,8,512]{0,2,1:T(8,128)(2,1)}), bf16[256,8,512]{0,2,1:T(8,128)(2,1)S(1)}, u32[]{:S(2)}, u32[]{:S(2)}) async-start(bf16[256,8,512]{0,2,1:T(8,128)(2,1)} %bitcast.189), calls=%async_computation.2 | async-start | bytes 4194304 | tf_op jit(solution)/shard_map/all_to_all | solution.py:50
  66.6 53.4 %all-to-all-start.4 = ((bf16[256,8,512]{0,2,1:T(8,128)(2,1)}), bf16[256,8,512]{0,2,1:T(8,128)(2,1)}, u32[]{:S(2)}, u32[]{:S(2)}) async-start(bf16[256,8,512]{0,2,1:T(8,128)(2,1)} %bitcast.184), calls=%async_computation.4 | async-start | bytes 4194304 | tf_op jit(solution)/shard_map/all_to_all | solution.py:53
  120.0 53.4 %all-to-all-start.5 = ((bf16[256,8,512]{0,2,1:T(8,128)(2,1)}), bf16[256,8,512]{0,2,1:T(8,128)(2,1)}, u32[]{:S(2)}, u32[]{:S(2)}) async-start(bf16[256,8,512]{0,2,1:T(8,128)(2,1)} %bitcast.185), calls=%async_computation.5 | async-start | bytes 4194304 | tf_op jit(solution)/shard_map/all_to_all | solution.py:54
  173.4 53.4 %all-to-all-start = ((bf16[256,8,512]{0,2,1:T(8,128)(2,1)}), bf16[256,8,512]{0,2,1:T(8,128)(2,1)}, u32[]{:S(2)}, u32[]{:S(2)}) async-start(bf16[256,8,512]{0,2,1:T(8,128)(2,1)} %bitcast.186), calls=%async_computation | async-start | bytes 4194304 | tf_op jit(solution)/shard_map/all_to_all | solution.py:51
  226.8 53.4 %all-to-all-start.1 = ((bf16[256,8,512]{0,2,1:T(8,128)(2,1)}), bf16[256,8,512]{0,2,1:T(8,128)(2,1)}, u32[]{:S(2)}, u32[]{:S(2)}) async-start(bf16[256,8,512]{0,2,1:T(8,128)(2,1)} %bitcast.187), calls=%async_computation.1 | async-start | bytes 4194304 | tf_op jit(solution)/shard_map/all_to_all | solution.py:49
  280.2 53.4 %all-to-all-start.3 = ((bf16[256,8,512]{0,2,1:T(8,128)(2,1)}), bf16[256,8,512]{0,2,1:T(8,128)(2,1)}, u32[]{:S(2)}, u32[]{:S(2)}) async-start(bf16[256,8,512]{0,2,1:T(8,128)(2,1)} %bitcast.182), calls=%async_computation.3 | async-start | bytes 4194304 | tf_op jit(solution)/shard_map/all_to_all | solution.py:52
  284.6 785.2 %reduce-scatter.2.cloned.1.call-start = ((), (), s32[]{:S(2)}) async-start(), calls=%async_computation.9 | async-start | bytes 7864320 | tf_op jit(solution)/shard_map/reduce_scatter | solution.py:122
  287.1 50.5 %collective-permute-start.1 = (bf16[2048,512]{1,0:T(8,128)(2,1)}, bf16[2048,512]{1,0:T(8,128)(2,1)}, u32[]{:S(2)}, u32[]{:S(2)}) collective-permute-start(bf16[2048,512]{1,0:T(8,128)(2,1)} %bitcast.194), channel_id=1, source_target_pairs={{0,8},{8,16},{16,24},{24,0},{1,9},{9,17},{17,25},{25,1},{2,10},{10... | collective-permute-start | bytes 6291464 | tf_op jit(solution)/shard_map/ppermute | solution.py:12
  292.5 10.3 copy-start.14
  292.5 89.2 %collective-permute-start.2 = (bf16[2048,512]{1,0:T(8,128)(2,1)}, bf16[2048,512]{1,0:T(8,128)(2,1)}, u32[]{:S(2)}, u32[]{:S(2)}) collective-permute-start(bf16[2048,512]{1,0:T(8,128)(2,1)} %bitcast.36), channel_id=1, source_target_pairs={{0,8},{8,16},{16,24},{24,0},{1,9},{9,17},{17,25},{25,1},{2,10},{10... | collective-permute-start | bytes 6291464 | tf_op jit(solution)/shard_map/ppermute | solution.py:12
  297.9 128.7 %collective-permute-start.3 = (bf16[2048,512]{1,0:T(8,128)(2,1)}, bf16[2048,512]{1,0:T(8,128)(2,1)}, u32[]{:S(2)}, u32[]{:S(2)}) collective-permute-start(bf16[2048,512]{1,0:T(8,128)(2,1)} %bitcast.39), channel_id=1, source_target_pairs={{0,8},{8,16},{16,24},{24,0},{1,9},{9,17},{17,25},{25,1},{2,10},{10... | collective-permute-start | bytes 6291464 | tf_op jit(solution)/shard_map/ppermute | solution.py:12
  302.3 168.7 %collective-permute-start = (bf16[2048,512]{1,0:T(8,128)(2,1)S(1)}, bf16[2048,512]{1,0:T(8,128)(2,1)}, u32[]{:S(2)}, u32[]{:S(2)}) collective-permute-start(bf16[2048,512]{1,0:T(8,128)(2,1)S(1)} %bitcast.192), channel_id=1, source_target_pairs={{0,8},{8,16},{16,24},{24,0},{1,9},{9,17},{17,25},{25,1},{2,10},{10... | collective-permute-start | bytes 6291464 | tf_op jit(solution)/shard_map/ppermute | solution.py:12
  501.8 9.6 copy-start.12
  533.0 11.3 %copy-start.3 = (bf16[4096,512]{0,1:T(8,128)(2,1)S(1)}, bf16[4096,512]{0,1:T(8,128)(2,1)}, u32[]{:S(2)}) copy-start(bf16[4096,512]{0,1:T(8,128)(2,1)} %get-tuple-element.466) | copy-start | bytes 12582916 | tf_op jit(solution)/shard_map/while
  533.0 11.3 %copy-start.4 = (bf16[4096,512]{0,1:T(8,128)(2,1)S(1)}, bf16[4096,512]{0,1:T(8,128)(2,1)}, u32[]{:S(2)}) copy-start(bf16[4096,512]{0,1:T(8,128)(2,1)} %get-tuple-element.467) | copy-start | bytes 12582916 | tf_op jit(solution)/shard_map/while
  578.3 12.7 %copy-start.8 = (bf16[3072,512]{0,1:T(8,128)(2,1)}, bf16[3072,512]{0,1:T(8,128)(2,1)S(1)}, u32[]{:S(2)}) copy-start(bf16[3072,512]{0,1:T(8,128)(2,1)S(1)} %pad_maximum_fusion.14) | copy-start | bytes 9437188 | tf_op jit(solution)/shard_map/while
  578.3 12.7 %copy-start = (bf16[1024,512]{0,1:T(8,128)(2,1)S(1)}, bf16[1024,512]{0,1:T(8,128)(2,1)}, u32[]{:S(2)}) copy-start(bf16[1024,512]{0,1:T(8,128)(2,1)} %get-tuple-element.391) | copy-start | bytes 3145732 | tf_op jit(solution)/shard_map/while
  578.3 12.7 %copy-start.1 = (bf16[1024,512]{0,1:T(8,128)(2,1)S(1)}, bf16[1024,512]{0,1:T(8,128)(2,1)}, u32[]{:S(2)}) copy-start(bf16[1024,512]{0,1:T(8,128)(2,1)} %get-tuple-element.390) | copy-start | bytes 3145732 | tf_op jit(solution)/shard_map/while
  578.3 12.7 %copy-start.2 = (bf16[1024,512]{0,1:T(8,128)(2,1)S(1)}, bf16[1024,512]{0,1:T(8,128)(2,1)}, u32[]{:S(2)}) copy-start(bf16[1024,512]{0,1:T(8,128)(2,1)} %get-tuple-element.392) | copy-start | bytes 3145732 | tf_op jit(solution)/shard_map/while
  591.0 1.2 copy-start.15
  591.3 19.7 %copy-start.5 = (bf16[3072,512]{0,1:T(8,128)(2,1)}, bf16[3072,512]{0,1:T(8,128)(2,1)S(1)}, u32[]{:S(2)}) copy-start(bf16[3072,512]{0,1:T(8,128)(2,1)S(1)} %pad_maximum_fusion.12) | copy-start | bytes 9437188 | tf_op jit(solution)/shard_map/while
  640.1 28.2 %copy-start.9 = (bf16[3072,512]{0,1:T(8,128)(2,1)S(1)}, bf16[3072,512]{0,1:T(8,128)(2,1)}, u32[]{:S(2)}) copy-start(bf16[3072,512]{0,1:T(8,128)(2,1)} %copy-done.8) | copy-start | bytes 9437188 | tf_op jit(solution)/shard_map/while
  668.3 10.7 copy-start.6
  678.9 17.9 %copy-start.10 = (bf16[4,128,512]{2,1,0:T(8,128)(2,1)S(1)}, bf16[4,128,512]{2,1,0:T(8,128)(2,1)}, u32[]{:S(2)}) copy-start(bf16[4,128,512]{2,1,0:T(8,128)(2,1)} %fusion.135) | copy-start | bytes 1572868 | tf_op jit(solution)/shard_map/while
  698.6 11.6 %copy-start.7 = (bf16[3072,512]{0,1:T(8,128)(2,1)S(1)}, bf16[3072,512]{0,1:T(8,128)(2,1)}, u32[]{:S(2)}) copy-start(bf16[3072,512]{0,1:T(8,128)(2,1)} %copy-done.5) | copy-start | bytes 9437188 | tf_op jit(solution)/shard_map/while
  720.7 1.7 copy-start.13
  722.5 9.5 copy-start.12
  753.7 11.3 %copy-start.3 = (bf16[4096,512]{0,1:T(8,128)(2,1)S(1)}, bf16[4096,512]{0,1:T(8,128)(2,1)}, u32[]{:S(2)}) copy-start(bf16[4096,512]{0,1:T(8,128)(2,1)} %get-tuple-element.466) | copy-start | bytes 12582916 | tf_op jit(solution)/shard_map/while
  753.7 11.3 %copy-start.4 = (bf16[4096,512]{0,1:T(8,128)(2,1)S(1)}, bf16[4096,512]{0,1:T(8,128)(2,1)}, u32[]{:S(2)}) copy-start(bf16[4096,512]{0,1:T(8,128)(2,1)} %get-tuple-element.467) | copy-start | bytes 12582916 | tf_op jit(solution)/shard_map/while
  799.0 12.7 %copy-start.8 = (bf16[3072,512]{0,1:T(8,128)(2,1)}, bf16[3072,512]{0,1:T(8,128)(2,1)S(1)}, u32[]{:S(2)}) copy-start(bf16[3072,512]{0,1:T(8,128)(2,1)S(1)} %pad_maximum_fusion.14) | copy-start | bytes 9437188 | tf_op jit(solution)/shard_map/while
  799.0 12.7 %copy-start = (bf16[1024,512]{0,1:T(8,128)(2,1)S(1)}, bf16[1024,512]{0,1:T(8,128)(2,1)}, u32[]{:S(2)}) copy-start(bf16[1024,512]{0,1:T(8,128)(2,1)} %get-tuple-element.391) | copy-start | bytes 3145732 | tf_op jit(solution)/shard_map/while
  799.0 12.7 %copy-start.1 = (bf16[1024,512]{0,1:T(8,128)(2,1)S(1)}, bf16[1024,512]{0,1:T(8,128)(2,1)}, u32[]{:S(2)}) copy-start(bf16[1024,512]{0,1:T(8,128)(2,1)} %get-tuple-element.390) | copy-start | bytes 3145732 | tf_op jit(solution)/shard_map/while
  799.0 12.7 %copy-start.2 = (bf16[1024,512]{0,1:T(8,128)(2,1)S(1)}, bf16[1024,512]{0,1:T(8,128)(2,1)}, u32[]{:S(2)}) copy-start(bf16[1024,512]{0,1:T(8,128)(2,1)} %get-tuple-element.392) | copy-start | bytes 3145732 | tf_op jit(solution)/shard_map/while
  811.7 1.2 copy-start.15
  812.0 19.7 %copy-start.5 = (bf16[3072,512]{0,1:T(8,128)(2,1)}, bf16[3072,512]{0,1:T(8,128)(2,1)S(1)}, u32[]{:S(2)}) copy-start(bf16[3072,512]{0,1:T(8,128)(2,1)S(1)} %pad_maximum_fusion.12) | copy-start | bytes 9437188 | tf_op jit(solution)/shard_map/while
  860.8 28.2 %copy-start.9 = (bf16[3072,512]{0,1:T(8,128)(2,1)S(1)}, bf16[3072,512]{0,1:T(8,128)(2,1)}, u32[]{:S(2)}) copy-start(bf16[3072,512]{0,1:T(8,128)(2,1)} %copy-done.8) | copy-start | bytes 9437188 | tf_op jit(solution)/shard_map/while
  889.0 10.7 copy-start.6
  899.6 17.9 %copy-start.10 = (bf16[4,128,512]{2,1,0:T(8,128)(2,1)S(1)}, bf16[4,128,512]{2,1,0:T(8,128)(2,1)}, u32[]{:S(2)}) copy-start(bf16[4,128,512]{2,1,0:T(8,128)(2,1)} %fusion.135) | copy-start | bytes 1572868 | tf_op jit(solution)/shard_map/while
  919.3 11.6 %copy-start.7 = (bf16[3072,512]{0,1:T(8,128)(2,1)S(1)}, bf16[3072,512]{0,1:T(8,128)(2,1)}, u32[]{:S(2)}) copy-start(bf16[3072,512]{0,1:T(8,128)(2,1)} %copy-done.5) | copy-start | bytes 9437188 | tf_op jit(solution)/shard_map/while
  941.4 1.7 copy-start.13
  955.4 1.6 copy-start.11
  1010.7 52.6 %all-to-all-start.7 = ((bf16[8,256,512]{2,1,0:T(8,128)(2,1)}), bf16[8,256,512]{2,1,0:T(8,128)(2,1)S(1)}, u32[]{:S(2)}, u32[]{:S(2)}) async-start(bf16[8,256,512]{2,1,0:T(8,128)(2,1)} %bitcast.198), calls=%async_computation.7 | async-start | bytes 4194304 | tf_op jit(solution)/shard_map/all_to_all | solution.py:115
Sparse Core Ops, SparseCore 0:
  955.6 70.2 reduce-scatter.1
where the time goes:
time: 1090 us; the launch traced here: 1080 us
  waiting for transfers between devices  393 us (36%)
  matrix products  389 us (36%)
  local copies, waits for them, and re-layouts  140 us (13%)
  blocking collectives  53.7 us (5%)
  starting transfers between devices  36.8 us (3%)
  loops' own time  27 us (2%)
  other arithmetic  26 us (2%)
  between operations  14.5 us (1%)
    dot_general x4, matrix products, attend_block(): jnp.einsum('qhd,khd->hqk', query_block, ktan_win, preferred_element_type=...  113 us
    ppermute x4, waiting for transfers between devices, shifted(): lax.ppermute(shard, axis, [(i, (i + by) % length) for i in range(length)])  101 us
    dot_general x4, matrix products, attend_block(): jnp.einsum('hqk,khd->qhd', tangent_low, value_win, preferred_element_type...  73.2 us
    sub x4, matrix products, attend_block(): raw_weights = jnp.exp(scores - row_max)  55 us
    all_to_all x1, blocking collectives, on_device(): lax.all_to_all(as_sent(output_h), 'head', split_axis=0, concat_axis=1, ti...  53.7 us
    dot_general x4, matrix products, attend_block(): jnp.einsum('hqk,khd->qhd', prob_low, vtan_win, preferred_element_type=jnp...  46.6 us
    dot_general x4, matrix products, attend_block(): jnp.einsum('qhd,khd->hqk', qtan_block, key_win, preferred_element_type=jn...  45.2 us
    all_to_all x1, waiting for transfers between devices, on_device(): lax.all_to_all(key_rows, 'head', split_axis=1, concat_axis=0, tiled=True)  45 us
  transfers between devices with their start and end apart: 12, of which 10 were waited for; matrix products, arithmetic and copies ran while one was open for 8% of the time, Pallas kernels for 0%

commit v1 on v0

v1 whole, which is shorter than its diff:
```python
import functools
import math

import jax
import jax.numpy as jnp
from jax import lax
from jax.experimental import pallas as pl
from jax.experimental.pallas import tpu as pltpu
from jax.sharding import PartitionSpec as P

HDIM = 128
CLIP = 1024
NT = (((1,), (1,)), ((), ()))


def attend_rows(query, qtan, wk, wv, scale):
    f32 = jnp.float32
    hdim = query.shape[1]
    scores = lax.dot_general(query, wk[:, :hdim], NT, preferred_element_type=f32)
    both = jnp.concatenate([qtan, query], axis=1)
    score_tan = lax.dot_general(both, wk[...], NT, preferred_element_type=f32)
    row_max = jnp.max(scores, axis=1, keepdims=True)
    weights = jnp.exp2((scores - row_max) * (scale * math.log2(math.e)))
    inverse = 1.0 / jnp.sum(weights, axis=1, keepdims=True)
    mean = jnp.sum(weights * score_tan, axis=1, keepdims=True) * inverse
    low = weights.astype(jnp.bfloat16)
    tan_low = (weights * (score_tan - mean)).astype(jnp.bfloat16)
    first = jnp.dot(low, wv[...], preferred_element_type=f32)
    second = jnp.dot(tan_low, wv[:, :hdim], preferred_element_type=f32)
    out = first[:, :hdim] * inverse
    tan = (first[:, hdim:] + second * scale) * inverse
    return out.astype(jnp.bfloat16), tan.astype(jnp.bfloat16)


def attention_kernel(
    clips_here, slots, q, qt, k, v, kt, vt, pk, pv, pkt, pvt, out, tan, wk, wv
):
    within, block = pl.program_id(1), pl.program_id(2)

    @pl.when(block == 0)
    def _():
        def fill(place, own, slot):
            def put(a, b, c, d):
                rows = pl.ds(pl.multiple_of(slot * CLIP, CLIP), CLIP)
                at = pl.ds(place * CLIP, CLIP)
                wk[at, :HDIM] = a[rows, :]
                wk[at, HDIM:] = b[rows, :]
                wv[at, :HDIM] = c[rows, :]
                wv[at, HDIM:] = d[rows, :]

            if own:
                put(k, kt, v, vt)
            else:
                put(pk, pkt, pv, pvt)

        fill(0, True, within)
        for place in (1, 2):
            slot = slots[within * 2 + place - 1]

            @pl.when(slot < clips_here)
            def _():
                fill(place, False, slot)

            @pl.when(slot >= clips_here)
            def _():
                fill(place, True, slot - clips_here)

    out[...], tan[...] = attend_rows(q[...], qt[...], wk, wv, HDIM**-0.5)


def attention(slots, query, qtan, own, prev):
    rows, cols = query.shape
    clips_here = rows // CLIP
    block_rows = min(256, CLIP)
    blocks = CLIP // block_rows
    row_spec = pl.BlockSpec((block_rows, HDIM), lambda h, c, b, s: (c * blocks + b, h))
    all_spec = pl.BlockSpec((rows, HDIM), lambda h, c, b, s: (0, h))
    shape = jax.ShapeDtypeStruct((rows, cols), jnp.bfloat16)
    return pl.pallas_call(
        functools.partial(attention_kernel, clips_here),
        out_shape=(shape, shape),
        grid_spec=pltpu.PrefetchScalarGridSpec(
            num_scalar_prefetch=1,
            grid=(cols // HDIM, clips_here, blocks),
            in_specs=[row_spec] * 2 + [all_spec] * 8,
            out_specs=[row_spec] * 2,
            scratch_shapes=[
                pltpu.VMEM((3 * CLIP, 2 * HDIM), jnp.bfloat16),
                pltpu.VMEM((3 * CLIP, 2 * HDIM), jnp.bfloat16),
            ],
        ),
        compiler_params=pltpu.CompilerParams(vmem_limit_bytes=60 * 1024 * 1024),
        cost_estimate=pl.CostEstimate(
            flops=12 * rows * cols * 3 * CLIP,
            bytes_accessed=12 * rows * cols * 2,
            transcendentals=rows * cols // HDIM * 3 * CLIP,
        ),
    )(slots, query, qtan, *own, *prev)


def on_device(
    queries, key_rows, value_rows, query_tangent, key_tangent, value_tangent, partners, cotangent
):
    clip_count = lax.axis_size("clip")
    ring = [(i, (i + 1) % clip_count) for i in range(clip_count)]

    def to_heads(a):
        return lax.all_to_all(a, "head", split_axis=1, concat_axis=0, tiled=True)

    own = tuple(to_heads(a) for a in (key_rows, value_rows, key_tangent, value_tangent))
    prev = tuple(lax.ppermute(a, "clip", ring) for a in own)
    query_h, qtan_h = to_heads(queries), to_heads(query_tangent)
    clips_here = query_h.shape[0] // CLIP
    first_clip = lax.axis_index("clip") * clips_here
    mine = lax.dynamic_slice_in_dim(partners, first_clip, clips_here, 0)
    slots = ((mine - first_clip + clips_here) % (clips_here * clip_count)).reshape(-1)
    output_h, tangent_h = attention(slots, query_h, qtan_h, own, prev)
    partial_term = lax.dot_general(
        cotangent, output_h, (((0,), (0,)), ((), ())), preferred_element_type=jnp.float32
    )
    weight_grad = lax.psum_scatter(partial_term, "clip", scatter_dimension=0, tiled=True)

    def to_tokens(a):
        return lax.all_to_all(a, "head", split_axis=0, concat_axis=1, tiled=True)

    return (to_tokens(output_h), to_tokens(tangent_h), weight_grad)


def solution(mesh):
    tokens = P(("clip", "head"), None)
    return jax.shard_map(
        on_device,
        mesh=mesh,
        in_specs=(tokens,) * 6 + (P(), P("clip", None)),
        out_specs=(tokens, tokens, P("clip", "head")),
        check_vma=False,
    )
```

time: 1090 us -> 688 us (0.63)
  matrix products: 389 us -> 12.1 us
  local copies, waits for them, and re-layouts: 140 us -> 20.9 us
  Pallas kernels: 0 us -> 87.9 us
  waiting for transfers between devices: 393 us -> 461 us
  loops' own time: 27 us -> 0 us
  other arithmetic: 26 us -> 0.08 us
    dot_general x20 -> x0, matrix products: 322 us -> none  [the longest x4 113 us: attend_block(): jnp.einsum('qhd,khd->hqk', query_block, ktan_win, preferred_element_type=...]
    pallas_call x0 -> x1, Pallas kernels: none -> 87.9 us  [attention(): pl.pallas_call(functools.partial(attention_kernel, clips_here), out_shape...]
    sub x4 -> x0, matrix products: 55 us -> none  [attend_block(): raw_weights = jnp.exp(scores - row_max)]
    while x69 -> x0, local copies, waits for them, and re-layouts: 44.2 us -> none  [the longest x5 25.8 us: on_device(): results = lax.map(one_clip, jnp.arange(clips_here, dtype=jnp.int32))]
    ppermute x4, waiting for transfers between devices: 101 us -> 135 us  [on_device(): prev = tuple((lax.ppermute(a, 'clip', ring) for a in own))]
    all_to_all x7, waiting for transfers between devices: 293 us -> 326 us  [the longest x6 281 us: to_heads(): return lax.all_to_all(a, 'head', split_axis=1, concat_axis=0, tiled=True)]
    unnamed x13 -> x17, local copies, waits for them, and re-layouts: 37.2 us -> 4.61 us
    another operation x1 -> x0, loops' own time: 27 us -> none  [on_device(): results = lax.map(one_clip, jnp.arange(clips_here, dtype=jnp.int32))]
  transfers between devices with their start and end apart: 12 -> 12, of which waited for: 10 -> 11; matrix products, arithmetic and copies ran while one was open for 8% -> 2% of each run, Pallas kernels for 0% -> 0%
where the time goes in v1:
time: 688 us; the launch traced here: 687 us
  waiting for transfers between devices  461 us (67%)
  Pallas kernels  87.9 us (13%)
  blocking collectives  53.7 us (8%)
  starting transfers between devices  36.8 us (5%)
  local copies, waits for them, and re-layouts  20.9 us (3%)
  between operations  14.1 us (2%)
  matrix products  12.1 us (2%)
    all_to_all x6, waiting for transfers between devices, to_heads(): return lax.all_to_all(a, 'head', split_axis=1, concat_axis=0, tiled=True)  281 us
    ppermute x4, waiting for transfers between devices, on_device(): prev = tuple((lax.ppermute(a, 'clip', ring) for a in own))  135 us
    pallas_call x1, Pallas kernels, attention(): pl.pallas_call(functools.partial(attention_kernel, clips_here), out_shape...  87.9 us
    all_to_all x1, blocking collectives, to_tokens(): return lax.all_to_all(a, 'head', split_axis=0, concat_axis=1, tiled=True)  53.7 us
    all_to_all x1, waiting for transfers between devices, to_tokens(): return lax.all_to_all(a, 'head', split_axis=0, concat_axis=1, tiled=True)  45.8 us
    all_to_all x6, starting transfers between devices, to_heads(): return lax.all_to_all(a, 'head', split_axis=1, concat_axis=0, tiled=True)  28.2 us
  transfers between devices with their start and end apart: 12, of which 11 were waited for; matrix products, arithmetic and copies ran while one was open for 2% of the time, Pallas kernels for 0%

profile of v1, /device:TPU:0, one launch (start us, length us, event | category | flops | bytes accessed | tf_op | source)
XLA Modules:
  0.0 687.0 jit_solution(10886780362915123259)
XLA Ops:
  7.2 3.1 copy.40
  10.3 0.0 copy-start
  10.3 6.5 all-to-all-start
  16.8 0.0 copy-done
  16.8 1.5 copy.38
  18.3 47.6 %all-to-all-done = bf16[256,8,512]{2,0,1:T(8,128)(2,1)} async-done(((bf16[256,8,512]{2,0,1:T(8,128)(2,1)}), bf16[256,8,512]{2,0,1:T(8,128)(2,1)}, u32[]{:S(2)}, u32[]{:S(2)}) %all-to-all-start) | async-done | bytes 2097184 | tf_op jit(solution)/shard_map/all_to_all | solution.py:108
  65.9 4.5 all-to-all-start.2
  70.4 0.0 copy-done.1
  70.4 1.5 copy.37
  71.9 47.5 %all-to-all-done.2 = bf16[256,8,512]{2,0,1:T(8,128)(2,1)} async-done(((bf16[256,8,512]{2,0,1:T(8,128)(2,1)}), bf16[256,8,512]{2,0,1:T(8,128)(2,1)}, u32[]{:S(2)}, u32[]{:S(2)}) %all-to-all-start.2) | async-done | bytes 2097184 | tf_op jit(solution)/shard_map/all_to_all | solution.py:108
  119.4 4.5 all-to-all-start.3
  123.9 0.0 copy-done.2
  123.9 1.5 copy.36
  125.4 47.5 %all-to-all-done.3 = bf16[256,8,512]{2,0,1:T(8,128)(2,1)} async-done(((bf16[256,8,512]{2,0,1:T(8,128)(2,1)}), bf16[256,8,512]{2,0,1:T(8,128)(2,1)}, u32[]{:S(2)}, u32[]{:S(2)}) %all-to-all-start.3) | async-done | bytes 2097184 | tf_op jit(solution)/shard_map/all_to_all | solution.py:108
  173.0 4.5 all-to-all-start.4
  177.5 0.0 copy-done.3
  177.5 1.6 copy.35
  179.1 47.4 %all-to-all-done.4 = bf16[256,8,512]{2,0,1:T(8,128)(2,1)} async-done(((bf16[256,8,512]{2,0,1:T(8,128)(2,1)}), bf16[256,8,512]{2,0,1:T(8,128)(2,1)}, u32[]{:S(2)}, u32[]{:S(2)}) %all-to-all-start.4) | async-done | bytes 2097184 | tf_op jit(solution)/shard_map/all_to_all | solution.py:108
  226.5 4.5 all-to-all-start.5
  231.0 0.0 copy-done.4
  231.0 1.5 copy.39
  232.5 47.5 %all-to-all-done.5 = bf16[256,8,512]{2,0,1:T(8,128)(2,1)} async-done(((bf16[256,8,512]{2,0,1:T(8,128)(2,1)}), bf16[256,8,512]{2,0,1:T(8,128)(2,1)}, u32[]{:S(2)}, u32[]{:S(2)}) %all-to-all-start.5) | async-done | bytes 2097184 | tf_op jit(solution)/shard_map/all_to_all | solution.py:108
  280.0 3.7 all-to-all-start.1
  283.8 0.0 reduce-scatter.2.cloned.1.call-start
  283.8 1.5 collective-permute-start.3
  285.4 1.5 collective-permute-start.2
  286.9 1.5 collective-permute-start.1
  288.4 0.5 collective-permute-start
  288.8 0.0 copy-done.7
  288.8 0.1 and_select_fusion
  288.9 0.1 copy.11
  289.0 0.6 reshape.33.slots
  289.6 43.1 %all-to-all-done.1 = bf16[256,8,512]{2,0,1:T(8,128)(2,1)S(1)} async-done(((bf16[256,8,512]{2,0,1:T(8,128)(2,1)}), bf16[256,8,512]{2,0,1:T(8,128)(2,1)S(1)}, u32[]{:S(2)}, u32[]{:S(2)}) %all-to-all-start.1) | async-done | bytes 2097184 | tf_op jit(solution)/shard_map/all_to_all | solution.py:108
  332.8 0.9 collective-permute-done.3.pvt
  333.6 44.9 %collective-permute-done.2.pkt = bf16[2048,512]{1,0:T(8,128)(2,1)} collective-permute-done((bf16[2048,512]{1,0:T(8,128)(2,1)}, bf16[2048,512]{1,0:T(8,128)(2,1)}, u32[]{:S(2)}, u32[]{:S(2)}) %collective-permute-start.2) | collective-permute-done | bytes 2097184 | tf_op jit(solution)/shard_map/ppermute | solution.py:111
  378.5 44.9 %collective-permute-done.1.pv = bf16[2048,512]{1,0:T(8,128)(2,1)} collective-permute-done((bf16[2048,512]{1,0:T(8,128)(2,1)}, bf16[2048,512]{1,0:T(8,128)(2,1)}, u32[]{:S(2)}, u32[]{:S(2)}) %collective-permute-start.1) | collective-permute-done | bytes 2097184 | tf_op jit(solution)/shard_map/ppermute | solution.py:111
  423.5 44.3 %collective-permute-done.pk = bf16[2048,512]{1,0:T(8,128)(2,1)} collective-permute-done((bf16[2048,512]{1,0:T(8,128)(2,1)}, bf16[2048,512]{1,0:T(8,128)(2,1)}, u32[]{:S(2)}, u32[]{:S(2)}) %collective-permute-start) | collective-permute-done | bytes 2097184 | tf_op jit(solution)/shard_map/ppermute | solution.py:111
  467.8 0.0 copy-done.5
  467.8 87.9 %shard_map.103 = (bf16[2048,512]{1,0:T(8,128)(2,1)}, bf16[2048,512]{1,0:T(8,128)(2,1)}) custom-call(s32[4]{0:T(128)} %reshape.33.slots, bf16[2048,512]{1,0:T(8,128)(2,1)} %bitcast.1.q, bf16[2048,512]{1,0:T(8,128)(2,1)} %bitcast.62, bf16[2048,512]{1,0:T(8,128)(2,1)} %bitcast.5.k, bf16[2048,512]{1,0:T(8,128)(2,1)} %bitcast.7.v, bf16[2048,512]{1,0:T(8,128)(2,1)} %bitcast.9.kt, ...), custom_call_target="tpu_custom_call" | custom-call | flops 38654705664 | bytes 25165824 | tf_op jit(solution)/shard_map/pallas_call | solution.py:79
  555.6 12.1 %convolution_bitcast_fusion = f32[3072,512]{0,1:T(8,128)} fusion(bf16[2048,512]{1,0:T(8,128)(2,1)} %get-tuple-element.5, bf16[2048,3072]{1,0:T(8,128)(2,1)} %param.15), kind=kOutput, calls=%fused_computation | convolution fusion | flops 6442450944 | bytes 20971520 | tf_op jit(solution)/shard_map/dot_general | solution.py:118
  567.7 0.0 reduce-scatter.2.cloned.1.call-update
  567.8 1.6 copy-done.6
  569.3 53.7 %all_to_all.152 = bf16[8,256,512]{2,1,0:T(8,128)(2,1)} all-to-all(bf16[8,256,512]{2,1,0:T(8,128)(2,1)S(1)} %bitcast.64), channel_id=1, replica_groups=mesh['clip'=4,'head'=8] {'head'}, dimensions={0} | all-to-all | bytes 4194304 | tf_op jit(solution)/shard_map/all_to_all | solution.py:124
  623.0 3.6 all-to-all-start.7
  626.6 3.2 copy.27
  629.8 45.8 %all-to-all-done.7 = bf16[8,256,512]{2,1,0:T(8,128)(2,1)S(1)} async-done(((bf16[8,256,512]{2,1,0:T(8,128)(2,1)}), bf16[8,256,512]{2,1,0:T(8,128)(2,1)S(1)}, u32[]{:S(2)}, u32[]{:S(2)}) %all-to-all-start.7) | async-done | bytes 2097184 | tf_op jit(solution)/shard_map/all_to_all | solution.py:124
  675.6 1.6 copy.28
  677.2 3.0 copy.20
  (8 shorter events, 0.0 us)
Async XLA Ops:
  10.3 6.5 copy-start
  10.3 55.6 %all-to-all-start = ((bf16[256,8,512]{2,0,1:T(8,128)(2,1)}), bf16[256,8,512]{2,0,1:T(8,128)(2,1)}, u32[]{:S(2)}, u32[]{:S(2)}) async-start(bf16[256,8,512]{2,0,1:T(8,128)(2,1)} %bitcast.53), calls=%async_computation | async-start | bytes 4194304 | tf_op jit(solution)/shard_map/all_to_all | solution.py:108
  65.9 4.5 copy-start.1
  65.9 53.5 %all-to-all-start.2 = ((bf16[256,8,512]{2,0,1:T(8,128)(2,1)}), bf16[256,8,512]{2,0,1:T(8,128)(2,1)}, u32[]{:S(2)}, u32[]{:S(2)}) async-start(bf16[256,8,512]{2,0,1:T(8,128)(2,1)} %bitcast.51), calls=%async_computation.2 | async-start | bytes 4194304 | tf_op jit(solution)/shard_map/all_to_all | solution.py:108
  119.4 4.5 copy-start.2
  119.4 53.5 %all-to-all-start.3 = ((bf16[256,8,512]{2,0,1:T(8,128)(2,1)}), bf16[256,8,512]{2,0,1:T(8,128)(2,1)}, u32[]{:S(2)}, u32[]{:S(2)}) async-start(bf16[256,8,512]{2,0,1:T(8,128)(2,1)} %bitcast.50), calls=%async_computation.3 | async-start | bytes 4194304 | tf_op jit(solution)/shard_map/all_to_all | solution.py:108
  173.0 4.5 copy-start.3
  173.0 53.5 %all-to-all-start.4 = ((bf16[256,8,512]{2,0,1:T(8,128)(2,1)}), bf16[256,8,512]{2,0,1:T(8,128)(2,1)}, u32[]{:S(2)}, u32[]{:S(2)}) async-start(bf16[256,8,512]{2,0,1:T(8,128)(2,1)} %bitcast.49), calls=%async_computation.4 | async-start | bytes 4194304 | tf_op jit(solution)/shard_map/all_to_all | solution.py:108
  226.5 4.5 copy-start.4
  226.5 53.5 %all-to-all-start.5 = ((bf16[256,8,512]{2,0,1:T(8,128)(2,1)}), bf16[256,8,512]{2,0,1:T(8,128)(2,1)}, u32[]{:S(2)}, u32[]{:S(2)}) async-start(bf16[256,8,512]{2,0,1:T(8,128)(2,1)} %bitcast.48), calls=%async_computation.5 | async-start | bytes 4194304 | tf_op jit(solution)/shard_map/all_to_all | solution.py:108
  280.0 8.8 %copy-start.7 = (s32[8,2]{0,1:T(2,128)S(1)}, s32[8,2]{0,1:T(2,128)}, u32[]{:S(2)}) copy-start(s32[8,2]{0,1:T(2,128)} %param.14) | copy-start | bytes 196
  280.0 52.7 %all-to-all-start.1 = ((bf16[256,8,512]{2,0,1:T(8,128)(2,1)}), bf16[256,8,512]{2,0,1:T(8,128)(2,1)S(1)}, u32[]{:S(2)}, u32[]{:S(2)}) async-start(bf16[256,8,512]{2,0,1:T(8,128)(2,1)} %bitcast.52), calls=%async_computation.1 | async-start | bytes 4194304 | tf_op jit(solution)/shard_map/all_to_all | solution.py:108
  283.8 393.4 %reduce-scatter.2.cloned.1.call-start = ((), (), s32[]{:S(2)}) async-start(), calls=%async_computation.9 | async-start | bytes 7864320 | tf_op jit(solution)/shard_map/reduce_scatter | solution.py:121
  283.8 49.8 %collective-permute-start.3 = (bf16[2048,512]{1,0:T(8,128)(2,1)}, bf16[2048,512]{1,0:T(8,128)(2,1)}, u32[]{:S(2)}, u32[]{:S(2)}) collective-permute-start(bf16[2048,512]{1,0:T(8,128)(2,1)} %bitcast.11.vt), channel_id=1, source_target_pairs={{0,8},{8,16},{16,24},{24,0},{1,9},{9,17},{17,25},{25,1},{2,10},{10... | collective-permute-start | bytes 6291464 | tf_op jit(solution)/shard_map/ppermute | solution.py:111
  285.4 93.2 %collective-permute-start.2 = (bf16[2048,512]{1,0:T(8,128)(2,1)}, bf16[2048,512]{1,0:T(8,128)(2,1)}, u32[]{:S(2)}, u32[]{:S(2)}) collective-permute-start(bf16[2048,512]{1,0:T(8,128)(2,1)} %bitcast.9.kt), channel_id=1, source_target_pairs={{0,8},{8,16},{16,24},{24,0},{1,9},{9,17},{17,25},{25,1},{2,10},{10... | collective-permute-start | bytes 6291464 | tf_op jit(solution)/shard_map/ppermute | solution.py:111
  286.9 136.6 %collective-permute-start.1 = (bf16[2048,512]{1,0:T(8,128)(2,1)}, bf16[2048,512]{1,0:T(8,128)(2,1)}, u32[]{:S(2)}, u32[]{:S(2)}) collective-permute-start(bf16[2048,512]{1,0:T(8,128)(2,1)} %bitcast.7.v), channel_id=1, source_target_pairs={{0,8},{8,16},{16,24},{24,0},{1,9},{9,17},{17,25},{25,1},{2,10},{10... | collective-permute-start | bytes 6291464 | tf_op jit(solution)/shard_map/ppermute | solution.py:111
  288.4 179.4 %collective-permute-start = (bf16[2048,512]{1,0:T(8,128)(2,1)}, bf16[2048,512]{1,0:T(8,128)(2,1)}, u32[]{:S(2)}, u32[]{:S(2)}) collective-permute-start(bf16[2048,512]{1,0:T(8,128)(2,1)} %bitcast.5.k), channel_id=1, source_target_pairs={{0,8},{8,16},{16,24},{24,0},{1,9},{9,17},{17,25},{25,1},{2,10},{10... | collective-permute-start | bytes 6291464 | tf_op jit(solution)/shard_map/ppermute | solution.py:111
  332.7 135.0 %copy-start.5 = (bf16[256,8,512]{2,0,1:T(8,128)(2,1)}, bf16[256,8,512]{2,0,1:T(8,128)(2,1)S(1)}, u32[]{:S(2)}) copy-start(bf16[256,8,512]{2,0,1:T(8,128)(2,1)S(1)} %all-to-all-done.1) | copy-start | bytes 6291460
  567.7 1.6 copy-start.6
  623.0 52.6 %all-to-all-start.7 = ((bf16[8,256,512]{2,1,0:T(8,128)(2,1)}), bf16[8,256,512]{2,1,0:T(8,128)(2,1)S(1)}, u32[]{:S(2)}, u32[]{:S(2)}) async-start(bf16[8,256,512]{2,1,0:T(8,128)(2,1)} %bitcast.63), calls=%async_computation.7 | async-start | bytes 4194304 | tf_op jit(solution)/shard_map/all_to_all | solution.py:124
Sparse Core Ops, SparseCore 0:
  567.9 70.2 reduce-scatter.1
